TPU v7x, 32 devices: a whole 2x2x4 slice. The times are simulated.
32 devices in a mesh: wide: 8 (over y, x, core), narrow: 4 (over z).
Axes of the slice: x: 2, y: 2, z: 4, core: 2. Of those that a mesh axis runs over, the one named last changes fastest.
Arguments:
- local_slopes: float32 [32, 512, 128], P(('wide', 'narrow')), may hold values from -0.25 to 0.25
- global_slopes: float32 [32, 512, 1024], P(('wide', 'narrow')), may hold values from -0.25 to 0.25
- residuals: float32 [32, 512], P(('wide', 'narrow')), may hold values from -6 to 6
- weights: float32 [32, 512], P(('wide', 'narrow')), may hold values from 0.1 to 10
- track_slot_count: int32 [32], P(('wide', 'narrow')), may hold values from 64 to 512
- windows: int32 [32], P(('wide', 'narrow')), may hold values from 0 to 3
Outputs:
- normal_matrix: float32 [4, 1024, 1024], P(None, 'narrow', 'wide')
- normal_rhs: float32 [4, 1024], P(None, 'narrow')
All inputs are finite; a program needn't handle non-finite values.
Results may differ from a plain program's by a relative error of at most 0.0003.
Values sent between devices are 32-bit elements; how exact they have to be, the bound alone decides.
A program may use at most 64 MiB of HBM per device.

v0:
```python
import functools
import jax
import jax.numpy as jnp
from jax import lax
from jax.experimental import pallas as pl
from jax.experimental.pallas import tpu as pltpu
from jax.sharding import PartitionSpec as P

WINDOW_PARAMS = 1024
NWIN = 4
LANES = 128
CHUNK = 64
AHEAD = 3
LAG = 2
MESH = pl.DeviceIdType.MESH
HIGHEST = lax.Precision.HIGHEST
HIGH = lax.Precision.HIGH


def tdot(left, right, precision=HIGHEST):
    return lax.dot_general(
        left,
        right,
        (((0,), (0,)), ((), ())),
        precision=precision,
        preferred_element_type=jnp.float32,
    )


def invert(c):
    size = c.shape[0]
    sub = lax.broadcasted_iota(jnp.int32, (8, size), 0)
    lane = lax.broadcasted_iota(jnp.int32, (8, size), 1)
    rows = [c[r:r + 8, :] for r in range(0, size, 8)]
    for k in range(0, size, 2):
        r, o = divmod(k, 8)
        left = [jnp.broadcast_to(x[:, k:k + 1], x.shape) for x in rows]
        right = [jnp.broadcast_to(x[:, k + 1:k + 2], x.shape) for x in rows]
        r0 = jnp.broadcast_to(rows[r][o:o + 1, :], (8, size))
        r1 = jnp.broadcast_to(rows[r][o + 1:o + 2, :], (8, size))
        a = jnp.broadcast_to(left[r][o:o + 1, :], (8, size))
        b_low = jnp.broadcast_to(left[r][o + 1:o + 2, :], (8, size))
        b = jnp.broadcast_to(right[r][o:o + 1, :], (8, size))
        d = jnp.broadcast_to(right[r][o + 1:o + 2, :], (8, size))
        inv = 1.0 / (a * d - b * b_low)
        here, after = lane == k, lane == k + 1
        r0 = jnp.where(here, 1.0, jnp.where(after, 0.0, r0))
        r1 = jnp.where(after, 1.0, jnp.where(here, 0.0, r1))
        p0 = (d * r0 - b * r1) * inv
        p1 = (a * r1 - b_low * r0) * inv
        pair = here | after
        rows = [jnp.where(pair, 0.0, x) - u * p0 - v * p1 for x, u, v in zip(rows, left, right)]
        rows[r] = jnp.where(sub == o, p0, jnp.where(sub == o + 1, p1, rows[r]))
    return jnp.concatenate(rows, axis=0)


def split(x):
    high = x.astype(jnp.bfloat16)
    return high, (x - high.astype(jnp.float32)).astype(jnp.bfloat16)


def bundle_kernel(count_ref, window_ref, local_ref, global_ref, resid_ref, weight_ref,
                  schur_ref, small_ref, high, low, u_high, u_low, x_high, x_low, gr):
    slots, params = global_ref.shape
    size = local_ref.shape[1]
    groups = params // LANES
    slot = lax.broadcasted_iota(jnp.int32, (1, slots), 1)
    root = jnp.sqrt(jnp.where(slot < count_ref[0], weight_ref[...], 0.0))
    root_col = jnp.broadcast_to(root, (LANES, slots)).T
    rs_col = jnp.broadcast_to(root * resid_ref[...], (LANES, slots)).T
    ls = local_ref[...] * root_col
    eye = (lax.broadcasted_iota(jnp.int32, (size, size), 0)
           == lax.broadcasted_iota(jnp.int32, (size, size), 1)).astype(jnp.float32)
    ls_t = ls.T
    inverse = invert(jnp.dot(ls_t, ls, precision=HIGHEST, preferred_element_type=jnp.float32) + eye)
    lr = jnp.sum(ls * rs_col, axis=0, keepdims=True)
    lr_col = jnp.broadcast_to(lr, (LANES, size)).T
    for g in range(groups):
        cols = slice(g * LANES, (g + 1) * LANES)
        gs = global_ref[:, cols] * root_col
        high[:, cols], low[:, cols] = split(gs)
        coupling = jnp.dot(ls_t, gs, precision=HIGHEST, preferred_element_type=jnp.float32)
        solved = jnp.dot(inverse, coupling, precision=HIGHEST, preferred_element_type=jnp.float32)
        u_high[:, cols], u_low[:, cols] = split(coupling)
        x_high[:, cols], x_low[:, cols] = split(solved)
        gr[g:g + 1, :] = (jnp.sum(gs * rs_col, axis=0, keepdims=True)
                          - jnp.sum(solved * lr_col, axis=0, keepdims=True))
    small_ref[:groups, :] = gr[...]
    small_ref[groups:, :] = (lax.broadcasted_iota(jnp.int32, (groups, LANES), 0)
                             == window_ref[0]).astype(jnp.float32)

    @pl.loop(0, groups)
    def _(i):
        cols = pl.ds(pl.multiple_of(i * LANES, LANES), LANES)

        def product(left, right):
            return lax.dot_general(left[:, cols], right[...], (((0,), (0,)), ((), ())),
                                   preferred_element_type=jnp.float32)

        gram = product(high, high) + (product(high, low) + product(low, high))
        taken = product(u_high, x_high) + (product(u_high, x_low) + product(u_low, x_high))
        schur_ref[cols, :] = gram - taken


def reduce_bundle(count, window, local_b, global_b, resid, weight):
    slots, params = global_b.shape
    size = local_b.shape[1]
    groups = params // LANES
    smem = pl.BlockSpec(memory_space=pltpu.SMEM)
    vmem = pl.BlockSpec(memory_space=pltpu.VMEM)
    bf16 = jnp.bfloat16
    return pl.pallas_call(
        bundle_kernel,
        out_shape=(jax.ShapeDtypeStruct((params, params), jnp.float32),
                   jax.ShapeDtypeStruct((2 * groups, LANES), jnp.float32)),
        in_specs=[smem, smem, vmem, vmem, vmem, vmem],
        out_specs=(vmem, vmem),
        scratch_shapes=[
            pltpu.VMEM((slots, params), bf16), pltpu.VMEM((slots, params), bf16),
            pltpu.VMEM((size, params), bf16), pltpu.VMEM((size, params), bf16),
            pltpu.VMEM((size, params), bf16), pltpu.VMEM((size, params), bf16),
            pltpu.VMEM((groups, LANES), jnp.float32),
        ],
        compiler_params=pltpu.CompilerParams(vmem_limit_bytes=24 * 1024 * 1024),
        name="bundle",
    )(count, window, local_b, global_b, resid, weight)


def spread_kernel(nq, nz, s_ref, small_ref, out_ref, rhs_ref,
                  recv, small, part, from_lo, from_hi, mirror, rsum, rrecv,
                  own_sem, send_sem, recv_sem, small_send, small_recv,
                  z_send, lo_sem, hi_sem, r_send, r_recv, m_send, m_recv):
    q = lax.axis_index("wide")
    z = lax.axis_index("narrow")
    chunks = recv.shape[1]
    half = nq // 2
    cuts = LANES // CHUNK
    per_z = nq // nz
    groups = small.shape[1] // 2

    def peer(step):
        return lax.rem(q + step, nq)

    barrier = pltpu.get_barrier_semaphore()
    for dz in range(nz):
        for step in range(nq):
            if dz or step:
                pl.semaphore_signal(barrier, inc=1, device_id=(peer(step), lax.rem(z + dz, nz)),
                                    device_id_type=MESH)
    pl.semaphore_wait(barrier, nq * nz - 1)

    def block_of(t, col):
        return lax.rem(col + lax.rem(t, half + 1), nq)

    def target(t):
        return block_of(t, q) // per_z

    def cut_of(t):
        return t // (half + 1)

    def piece(t, col):
        row = block_of(t, col) * LANES + cut_of(t) * CHUNK
        return s_ref.at[pl.ds(pl.multiple_of(row, CHUNK), CHUNK), pl.ds(pl.multiple_of(col * LANES, LANES), LANES)]

    def plane_copy(t, step):
        return pltpu.make_async_remote_copy(
            src_ref=piece(t, peer(step)), dst_ref=recv.at[nq - step, t],
            send_sem=send_sem.at[step, t], recv_sem=recv_sem.at[nq - step, t],
            device_id=(peer(step), z), device_id_type=MESH)

    def own_copy(t):
        return pltpu.make_async_copy(piece(t, q), recv.at[0, t], own_sem.at[t])

    def small_copy(step):
        return pltpu.make_async_remote_copy(
            src_ref=small_ref, dst_ref=small.at[nq - step],
            send_sem=small_send.at[step], recv_sem=small_recv.at[nq - step],
            device_id=(peer(step), z), device_id_type=MESH)

    def up_copy(t):
        return pltpu.make_async_remote_copy(
            src_ref=part.at[t], dst_ref=from_lo.at[t], send_sem=z_send.at[t], recv_sem=lo_sem.at[t],
            device_id=(q, lax.min(z + 1, nz - 1)), device_id_type=MESH)

    def down_copy(t):
        return pltpu.make_async_remote_copy(
            src_ref=part.at[t], dst_ref=from_hi.at[t], send_sem=z_send.at[t], recv_sem=hi_sem.at[t],
            device_id=(q, lax.max(z - 1, 0)), device_id_type=MESH)

    def rhs_copy(step):
        return pltpu.make_async_remote_copy(
            src_ref=rsum, dst_ref=rrecv.at[nz - step],
            send_sem=r_send.at[step], recv_sem=r_recv.at[nz - step],
            device_id=(q, lax.rem(z + step, nz)), device_id_type=MESH)

    def mirror_copy(t):
        d = lax.rem(t, half + 1)
        return pltpu.make_async_remote_copy(
            src_ref=part.at[t], dst_ref=mirror.at[t], send_sem=m_send.at[t], recv_sem=m_recv.at[t],
            device_id=(lax.rem(q + d, nq), q // per_z), device_id_type=MESH)

    order = sorted(range(1, nq), key=lambda step: -min(step, nq - step))

    def send_chunk(t):
        for step in order:
            plane_copy(t, step).start()
        own_copy(t).start()

    for step in order:
        small_copy(step).start()
    for t in range(AHEAD):
        send_chunk(t)
    small[0] = small_ref[...]
    for step in range(1, nq):
        small_copy(nq - step).wait_recv()
    for w in range(NWIN):
        total = jnp.zeros((groups, LANES), jnp.float32)
        for s in range(nq):
            total = total + small[s, groups + w:groups + w + 1, :] * small[s, :groups, :]
        rsum[w] = total
    for step in range(1, nz):
        rhs_copy(step).start()

    def relay(t, hop):
        n = target(t)
        if hop == 0:
            @pl.when((z == 0) & (n > 0))
            def _():
                up_copy(t).start()

            @pl.when((z == nz - 1) & (n < nz - 1))
            def _():
                down_copy(t).start()
        else:
            @pl.when((z == hop) & (n > z))
            def _():
                up_copy(t).wait_recv()
                part[t] = part[t] + from_lo[t]
                up_copy(t).start()

            @pl.when((z == nz - 1 - hop) & (n < z))
            def _():
                down_copy(t).wait_recv()
                part[t] = part[t] + from_hi[t]
                down_copy(t).start()

    def finish(t):
        @pl.when(target(t) == z)
        def _():
            @pl.when(z > 0)
            def _():
                up_copy(t).wait_recv()
                part[t] = part[t] + from_lo[t]

            @pl.when(z < nz - 1)
            def _():
                down_copy(t).wait_recv()
                part[t] = part[t] + from_hi[t]
            d = lax.rem(t, half + 1)

            @pl.when((d > 0) & (d < half))
            def _():
                mirror_copy(t).start()
            row = lax.rem(block_of(t, q), per_z) * LANES + cut_of(t) * CHUNK
            out_ref[:, pl.ds(pl.multiple_of(row, CHUNK), CHUNK), :] = part[t]

    def body(t, carry):
        @pl.when(t + AHEAD < chunks)
        def _():
            send_chunk(t + AHEAD)

        @pl.when(t < chunks)
        def _():
            own_copy(t).wait()
            for step in order:
                plane_copy(t, nq - step).wait_recv()
            for w in range(NWIN):
                total = jnp.zeros((CHUNK, LANES), jnp.float32)
                for s in range(nq):
                    total = total + small[s, groups + w:groups + w + 1, :] * recv[s, t]
                part[t, w] = total
            relay(t, 0)
        for hop in range(1, nz - 1):
            late = t - LAG * hop

            @pl.when((late >= 0) & (late < chunks))
            def _(late=late, hop=hop):
                relay(late, hop)
        last = t - LAG * (nz - 1)

        @pl.when(last >= 0)
        def _():
            finish(last)
        return carry

    lax.fori_loop(0, chunks + LAG * (nz - 1), body, 0)

    for d in range(1, half):
        source = lax.rem(q + nq - d, nq)

        @pl.when(source // per_z == z)
        def _(d=d, source=source):
            for cut in range(cuts):
                mirror_copy(cut * (half + 1) + d).wait_recv()
            row = lax.rem(source, per_z) * LANES
            for w in range(NWIN):
                block = jnp.concatenate([mirror[cut * (half + 1) + d, w] for cut in range(cuts)], axis=0)
                out_ref[w, pl.ds(pl.multiple_of(row, LANES), LANES), :] = block.T

    for step in range(1, nz):
        rhs_copy(nz - step).wait_recv()
    total = rsum[...]
    for step in range(1, nz):
        total = total + rrecv[step]
    rhs_ref[...] = total

    for step in range(1, nq):
        small_copy(step).wait_send()
    for step in range(1, nz):
        rhs_copy(step).wait_send()

    def drain(t, carry):
        for step in range(1, nq):
            plane_copy(t, step).wait_send()
        d = lax.rem(t, half + 1)

        @pl.when(target(t) != z)
        def _():
            up_copy(t).wait_send()

        @pl.when((target(t) == z) & (d > 0) & (d < half))
        def _():
            mirror_copy(t).wait_send()
        return carry

    lax.fori_loop(0, chunks, drain, 0)


def spread(nq, nz, schur, small):
    params = schur.shape[0]
    groups = params // LANES
    chunks = (nq // 2 + 1) * (LANES // CHUNK)
    block = pltpu.VMEM((chunks, NWIN, CHUNK, LANES), jnp.float32)
    dma = pltpu.SemaphoreType.DMA
    return pl.pallas_call(
        functools.partial(spread_kernel, nq, nz),
        out_shape=(jax.ShapeDtypeStruct((NWIN, params // nz, LANES), jnp.float32),
                   jax.ShapeDtypeStruct((NWIN, groups, LANES), jnp.float32)),
        in_specs=[pl.BlockSpec(memory_space=pl.ANY), pl.BlockSpec(memory_space=pltpu.VMEM)],
        out_specs=(pl.BlockSpec(memory_space=pltpu.VMEM), pl.BlockSpec(memory_space=pltpu.VMEM)),
        scratch_shapes=[
            pltpu.VMEM((nq, chunks, CHUNK, LANES), jnp.float32),
            pltpu.VMEM((nq, 2 * groups, LANES), jnp.float32),
            block, block, block, block,
            pltpu.VMEM((NWIN, groups, LANES), jnp.float32),
            pltpu.VMEM((nz, NWIN, groups, LANES), jnp.float32),
            dma((chunks,)), dma((nq, chunks)), dma((nq, chunks)), dma((nq,)), dma((nq,)),
            dma((chunks,)), dma((chunks,)), dma((chunks,)), dma((nz,)), dma((nz,)),
            dma((chunks,)), dma((chunks,)),
        ],
        compiler_params=pltpu.CompilerParams(
            collective_id=0, has_side_effects=True, vmem_limit_bytes=40 * 1024 * 1024),
        name="spread",
    )(schur, small)


def reduced_bundle(local_b, global_b, resid_b, weight_b, count):
    measure_slot, local_param = local_b.shape
    slots = jnp.arange(measure_slot, dtype=jnp.int32)
    live = jnp.where(slots < count, weight_b, jnp.float32(0.0))
    root = jnp.sqrt(live)[:, None]
    ls = local_b * root
    gs = global_b * root
    rs = resid_b[:, None] * root
    curv = tdot(ls, ls) + jnp.eye(local_param, dtype=jnp.float32)
    coupling = tdot(ls, gs)
    lr = tdot(ls, rs)
    gr = tdot(gs, rs)[:, 0]
    factor = jnp.linalg.cholesky(curv)
    solved_all = jax.scipy.linalg.cho_solve((factor, True), jnp.concatenate([coupling, lr], axis=1))
    solved, solved_rhs = solved_all[:, :-1], solved_all[:, -1:]
    schur = tdot(gs, gs, HIGH) - tdot(coupling, solved, HIGH)
    reduced = gr - tdot(coupling, solved_rhs)[:, 0]
    return schur, reduced


def on_device(local_slopes, global_slopes, residuals, weights, track_slot_count, windows):
    nq, nz = lax.axis_size("wide"), lax.axis_size("narrow")
    slots, params = global_slopes.shape[1:]
    owned = params // nz
    z = lax.axis_index("narrow")
    if params // nq == LANES and local_slopes.shape[2] == LANES and owned % LANES == 0 and nq % 2 == 0 and nz > 1:
        schur, small = reduce_bundle(track_slot_count, windows, local_slopes[0], global_slopes[0],
                                     residuals, weights)
        matrix, rhs = spread(nq, nz, schur, small)
        return matrix, lax.dynamic_slice_in_dim(rhs.reshape(NWIN, params), z * owned, owned, 1)
    schur, reduced = reduced_bundle(
        local_slopes[0], global_slopes[0], residuals[0], weights[0], track_slot_count[0])
    picks = (windows[0] == jnp.arange(NWIN, dtype=jnp.int32)).astype(jnp.float32)
    rhs_whole = lax.psum(picks[:, None] * reduced[None], ("wide", "narrow"))
    normal_rhs = lax.dynamic_slice_in_dim(rhs_whole, z * owned, owned, 1)
    received = lax.all_to_all(schur[None], "wide", split_axis=2, concat_axis=0, tiled=True)
    all_picks = lax.all_gather(picks, "wide", axis=0)
    partial_value = jnp.einsum("bw,bij->wij", all_picks, received, precision=HIGHEST,
                               preferred_element_type=jnp.float32)
    return lax.psum_scatter(partial_value, "narrow", scatter_dimension=1, tiled=True), normal_rhs


def solution(mesh):
    in_specs = (
        P(("wide", "narrow"), None, None),
        P(("wide", "narrow"), None, None),
        P(("wide", "narrow"), None),
        P(("wide", "narrow"), None),
        P(("wide", "narrow")),
        P(("wide", "narrow")),
    )
    out_specs = (P(None, "narrow", "wide"), P(None, "narrow"))
    return jax.shard_map(
        on_device, mesh=mesh, in_specs=in_specs, out_specs=out_specs, check_vma=False
    )
```

profile of v0, /device:TPU:31, one launch (start us, length us, event | category | flops | bytes accessed | tf_op | source)
XLA Modules:
  0.0 85.8 jit_solution(18404435425710565783)
XLA Ops:
  1.9 0.0 copy-start
  1.9 1.6 %copy-done = f32[1,512,1024]{2,1,0:T(8,128)S(1)} copy-done((f32[1,512,1024]{2,1,0:T(8,128)S(1)}, f32[1,512,1024]{2,1,0:T(8,128)}, u32[]{:S(2)}) %copy-start) | copy-done | bytes 2097176
  3.5 0.0 copy-start.1
  3.5 0.9 %copy-done.1 = f32[1,512,128]{2,1,0:T(8,128)S(1)} copy-done((f32[1,512,128]{2,1,0:T(8,128)S(1)}, f32[1,512,128]{2,1,0:T(8,128)}, u32[]{:S(2)}) %copy-start.1) | copy-done | bytes 262168
  4.5 0.0 copy-start.2
  4.5 0.7 copy-done.2
  5.1 0.0 copy-start.3
  5.1 0.7 copy-done.3
  5.8 21.1 %bundle.1 = (f32[1024,1024]{1,0:T(8,128)S(1)}, f32[16,128]{1,0:T(8,128)S(1)}) custom-call(s32[1]{0:T(128)S(6)} %copy.12.count_ref, s32[1]{0:T(128)S(6)} %copy.13.window_ref, f32[512,128]{1,0:T(8,128)S(1)} %bitcast.7, f32[512,1024]{1,0:T(8,128)S(1)} %bitcast.6, f32[1,512]{1,0:T(1,128)S(1)} %copy-done.2, f32[1,512]{1,0:T(1,128)S(1)} %copy-done.3), custom_call_target="tpu_custom_call" | custom-call | tf_op jit(solution)/shard_map/bundle/pallas_call | solution.py:112
  27.0 57.4 %spread.1 = (f32[4,256,128]{2,1,0:T(8,128)S(1)}, f32[4,8,128]{2,1,0:T(8,128)S(1)}) custom-call(f32[1024,1024]{1,0:T(8,128)S(1)} %get-tuple-element.6.s_ref, f32[16,128]{1,0:T(8,128)S(1)} %get-tuple-element.7.small_ref), custom_call_target="tpu_custom_call" | custom-call | tf_op jit(solution)/shard_map/spread/pallas_call | solution.py:345
  84.4 0.6 constant_dynamic-slice_fusion
  85.0 0.8 copy.14
  (1 shorter events, 0.0 us)
Async XLA Ops:
  1.9 1.6 %copy-start = (f32[1,512,1024]{2,1,0:T(8,128)S(1)}, f32[1,512,1024]{2,1,0:T(8,128)}, u32[]{:S(2)}) copy-start(f32[1,512,1024]{2,1,0:T(8,128)} %param.7) | copy-start | bytes 6291460
  3.5 0.9 %copy-start.1 = (f32[1,512,128]{2,1,0:T(8,128)S(1)}, f32[1,512,128]{2,1,0:T(8,128)}, u32[]{:S(2)}) copy-start(f32[1,512,128]{2,1,0:T(8,128)} %param.6) | copy-start | bytes 786436
  4.5 0.7 copy-start.2
  5.1 0.7 copy-start.3
where the time goes:
time: 86 us; the launch traced here: 85.8 us
  Pallas kernels  78.5 us (91%)
  local copies, waits for them, and re-layouts  5.29 us (6%)
  between operations  1.96 us (2%)
    pallas_call x1, Pallas kernels, spread(): pl.pallas_call(functools.partial(spread_kernel, nq, nz), out_shape=(jax.S...  57.4 us
    pallas_call x1, Pallas kernels, reduce_bundle(): pl.pallas_call(bundle_kernel, out_shape=(jax.ShapeDtypeStruct((params, pa...  21.1 us
    unnamed x10, local copies, waits for them, and re-layouts  4.69 us

commit v1 on v0

v1 whole, which is shorter than its diff:
```python
import functools
import jax
import jax.numpy as jnp
from jax import lax
from jax.experimental import pallas as pl
from jax.experimental.pallas import tpu as pltpu
from jax.sharding import PartitionSpec as P

WINDOW_PARAMS = 1024
NWIN = 4
LANES = 128
SUB = 8
PANEL = 64
CUT = 64
AHEAD = 2
LAG = 1
MESH = pl.DeviceIdType.MESH
HIGHEST = lax.Precision.HIGHEST
HIGH = lax.Precision.HIGH


def tdot(left, right, precision=HIGHEST):
    return lax.dot_general(
        left,
        right,
        (((0,), (0,)), ((), ())),
        precision=precision,
        preferred_element_type=jnp.float32,
    )


def eliminate(rows, base):
    size = rows[0].shape[1]
    sub = lax.broadcasted_iota(jnp.int32, (SUB, size), 0)
    lane = lax.broadcasted_iota(jnp.int32, (SUB, size), 1)

    def row(x, k):
        return jnp.broadcast_to(x[k:k + 1, :], (SUB, size))

    for r in range(len(rows)):
        first = base + SUB * r
        cols = [[jnp.broadcast_to(x[:, first + j:first + j + 1], (SUB, size)) for j in range(SUB)] for x in rows]
        pivot, panel = list(cols[r]), rows[r]
        for k in range(0, SUB, 2):
            u, v = pivot[k], pivot[k + 1]
            a, c, b, d = row(u, k), row(u, k + 1), row(v, k), row(v, k + 1)
            inv = 1.0 / (a * d - b * c)

            def step(x, here=None, after=None):
                r0, r1 = row(x, k), row(x, k + 1)
                if here is not None:
                    r0 = jnp.where(here, 1.0, jnp.where(after, 0.0, r0))
                    r1 = jnp.where(after, 1.0, jnp.where(here, 0.0, r1))
                    x = jnp.where(here | after, 0.0, x)
                p0 = (d * r0 - b * r1) * inv
                p1 = (a * r1 - c * r0) * inv
                x = x - u * p0 - v * p1
                return jnp.where(sub == k, p0, jnp.where(sub == k + 1, p1, x))

            for j in range(k + 2, SUB):
                pivot[j] = step(pivot[j])
            panel = step(panel, lane == first + k, lane == first + k + 1)
        inside = (lane >= first) & (lane < first + SUB)
        heads = [row(panel, j) for j in range(SUB)]
        for i in range(len(rows)):
            if i != r:
                t = [cols[i][j] * heads[j] for j in range(SUB)]
                rows[i] = jnp.where(inside, 0.0, rows[i]) - (
                    ((t[0] + t[1]) + (t[2] + t[3])) + ((t[4] + t[5]) + (t[6] + t[7])))
        rows[r] = panel
    return jnp.concatenate(rows, axis=0)


def invert(c):
    size = c.shape[0]
    lane = lax.broadcasted_iota(jnp.int32, (1, size), 1)
    for base in range(0, size, PANEL):
        end = base + PANEL
        panel = eliminate([c[i:i + SUB, :] for i in range(base, end, SUB)], base)

        def framed(above, below):
            return jnp.concatenate([x for x in (above, panel, below) if x.shape[0]], axis=0)

        heads = framed(jnp.zeros((base, size), jnp.float32), jnp.zeros((size - end, size), jnp.float32))
        taken = jnp.dot(c, heads, precision=HIGHEST, preferred_element_type=jnp.float32)
        rest = jnp.where((lane >= base) & (lane < end), 0.0, c) - taken
        c = framed(rest[:base, :], rest[end:, :])
    return c


def split(x):
    high = x.astype(jnp.bfloat16)
    return high, (x - high.astype(jnp.float32)).astype(jnp.bfloat16)


def product(left, right):
    return lax.dot_general(left, right, (((0,), (0,)), ((), ())), preferred_element_type=jnp.float32)


def three(left_high, left_low, right_high, right_low):
    return product(left_high, right_high) + (product(left_high, right_low) + product(left_low, right_high))


def assemble_kernel(nq, nz, count_ref, window_ref, local_hbm, global_hbm, resid_hbm, weight_hbm,
                    out_ref, rhs_ref,
                    ls_ref, gs_ref, resid_ref, weight_ref, high, low, u_ref, u_high, u_low, x_high, x_low,
                    s_ref, own, recv, small, part, from_lo, from_hi, mirror, rsum, rrecv,
                    in_sem, send_sem, recv_sem, small_send, small_recv,
                    z_send, lo_sem, hi_sem, r_send, r_recv, m_send, m_recv):
    q = lax.axis_index("wide")
    z = lax.axis_index("narrow")
    slots, params = gs_ref.shape
    size = ls_ref.shape[1]
    groups = params // LANES
    cuts = LANES // CUT
    extra = cuts * nz
    chip, core = q // 2, lax.rem(q, 2)
    steps = 2 * nz

    def peer(step):
        return lax.rem(q + step, nq)

    wide = params // 4
    loads = [pltpu.make_async_copy(weight_hbm, weight_ref, in_sem.at[0]),
             pltpu.make_async_copy(resid_hbm, resid_ref, in_sem.at[1]),
             pltpu.make_async_copy(local_hbm, ls_ref, in_sem.at[2])]
    loads += [pltpu.make_async_copy(global_hbm.at[:, i * wide:(i + 1) * wide], gs_ref.at[:, i * wide:(i + 1) * wide],
                                    in_sem.at[3 + i]) for i in range(4)]
    for copy in loads:
        copy.start()
    barrier = pltpu.get_barrier_semaphore()
    for dz in range(nz):
        for step in range(nq):
            if dz or step:
                pl.semaphore_signal(barrier, inc=1, device_id=(peer(step), lax.rem(z + dz, nz)),
                                    device_id_type=MESH)
    for copy in loads:
        copy.wait()

    slot = lax.broadcasted_iota(jnp.int32, (1, slots), 1)
    root = jnp.sqrt(jnp.where(slot < count_ref[0], weight_ref[...], 0.0))
    root_col = jnp.broadcast_to(root, (LANES, slots)).T
    rs_col = jnp.broadcast_to(root * resid_ref[...], (LANES, slots)).T
    ls = ls_ref[...] * root_col
    ls_t = ls.T
    eye = (lax.broadcasted_iota(jnp.int32, (size, size), 0)
           == lax.broadcasted_iota(jnp.int32, (size, size), 1)).astype(jnp.float32)
    curv = jnp.dot(ls_t, ls, precision=HIGHEST, preferred_element_type=jnp.float32) + eye
    lr = jnp.sum(ls * rs_col, axis=0, keepdims=True)
    lr_col = jnp.broadcast_to(lr, (LANES, size)).T
    ls_high, ls_low = split(ls_t)
    for g in range(groups):
        cols = slice(g * LANES, (g + 1) * LANES)
        gs = gs_ref[:, cols] * root_col
        gs_high, gs_low = split(gs)
        high[:, cols], low[:, cols] = gs_high, gs_low
        own[g:g + 1, :] = jnp.sum(gs * rs_col, axis=0, keepdims=True)
    inverse = invert(curv)
    wide = 2 * LANES
    for g in range(0, params, wide):
        cols = slice(g, g + wide)
        coupling = (jnp.dot(ls_high, high[:, cols], preferred_element_type=jnp.float32)
                    + (jnp.dot(ls_high, low[:, cols], preferred_element_type=jnp.float32)
                       + jnp.dot(ls_low, high[:, cols], preferred_element_type=jnp.float32)))
        u_ref[:, cols] = coupling
        u_high[:, cols], u_low[:, cols] = split(coupling)
    for g in range(0, params, wide):
        cols = slice(g, g + wide)
        solved = jnp.dot(inverse, u_ref[:, cols], precision=HIGHEST, preferred_element_type=jnp.float32)
        x_high[:, cols], x_low[:, cols] = split(solved)
        for h in range(2):
            r = g // LANES + h
            own[r:r + 1, :] = own[r:r + 1, :] - jnp.sum(
                solved[:, h * LANES:(h + 1) * LANES] * lr_col, axis=0, keepdims=True)
    own[groups:, :] = (lax.broadcasted_iota(jnp.int32, (groups, LANES), 0) == window_ref[0]).astype(jnp.float32)

    orders = [sorted(range(nz), key=lambda a: (-abs(a - i), a if i >= nz // 2 else -a)) for i in range(nz)]

    def goal(k):
        a = jnp.int32(0)
        for i in range(nz):
            for j in range(nz):
                a = a + jnp.where((z == i) & (k == j), orders[i][j], 0)
        return a

    def place(a):
        k = jnp.int32(0)
        for i in range(nz):
            for j in range(nz):
                k = k + jnp.where((z == i) & (a == orders[i][j]), j, 0)
        return k

    late = cuts * place(chip) + cuts

    def chunk(i):
        plain = jnp.where(i > late, i - 1, i)
        k = jnp.minimum(plain // cuts, nz - 1)
        a = jnp.where(i == late, chip, goal(k))
        return jnp.where(i == late, extra, cuts * a + lax.rem(plain, cuts)), a

    def turn(col, a):
        return jnp.where(col // 2 <= a, lax.rem(col, 2), 1 - lax.rem(col, 2))

    def corner(t, col):
        a = jnp.minimum(t // cuts, nz - 1)
        row = (2 * a + turn(col, a)) * LANES + lax.rem(t, cuts) * CUT
        side = lax.rem(col, 2)
        row = jnp.where(t == extra, (2 * (col // 2) + 1) * LANES + side * CUT, row)
        left = jnp.where(t == extra, col - side, col) * LANES
        return pl.ds(pl.multiple_of(row, CUT), CUT), pl.ds(pl.multiple_of(left, LANES), LANES)

    def plane_copy(t, step):
        rows, cols = corner(t, peer(step))
        return pltpu.make_async_remote_copy(
            src_ref=s_ref.at[rows, cols], dst_ref=recv.at[nq - step, t],
            send_sem=send_sem.at[step, t], recv_sem=recv_sem.at[nq - step, t],
            device_id=(peer(step), z), device_id_type=MESH)

    def small_copy(step):
        return pltpu.make_async_remote_copy(
            src_ref=own, dst_ref=small.at[nq - step],
            send_sem=small_send.at[step], recv_sem=small_recv.at[nq - step],
            device_id=(peer(step), z), device_id_type=MESH)

    def up_copy(t):
        return pltpu.make_async_remote_copy(
            src_ref=part.at[t], dst_ref=from_lo.at[t], send_sem=z_send.at[t], recv_sem=lo_sem.at[t],
            device_id=(q, lax.min(z + 1, nz - 1)), device_id_type=MESH)

    def down_copy(t):
        return pltpu.make_async_remote_copy(
            src_ref=part.at[t], dst_ref=from_hi.at[t], send_sem=z_send.at[t], recv_sem=hi_sem.at[t],
            device_id=(q, lax.max(z - 1, 0)), device_id_type=MESH)

    def rhs_copy(step):
        return pltpu.make_async_remote_copy(
            src_ref=rsum, dst_ref=rrecv.at[nz - step],
            send_sem=r_send.at[step], recv_sem=r_recv.at[nz - step],
            device_id=(q, lax.rem(z + step, nz)), device_id_type=MESH)

    def mirror_copy(cut):
        return pltpu.make_async_remote_copy(
            src_ref=part.at[cuts * z + cut], dst_ref=mirror.at[cut], send_sem=m_send.at[cut], recv_sem=m_recv.at[cut],
            device_id=(2 * z + turn(q, z), chip), device_id_type=MESH)

    def swap_copy(cut):
        return pltpu.make_async_remote_copy(
            src_ref=part.at[extra], dst_ref=mirror.at[cut], send_sem=m_send.at[cut], recv_sem=m_recv.at[cut],
            device_id=(q + 1 - 2 * core, z), device_id_type=MESH)

    order = sorted(range(1, nq), key=lambda step: -min(step, nq - step))
    pl.semaphore_wait(barrier, nq * nz - 1)
    for step in order:
        small_copy(step).start()

    def send(i):
        a, h = goal(i // 2), lax.rem(i, 2)
        block = pl.ds(pl.multiple_of((2 * a + h) * LANES, LANES), LANES)
        s_ref[block, :] = (three(high[:, block], low[:, block], high[...], low[...])
                           - three(u_high[:, block], u_low[:, block], x_high[...], x_low[...]))
        for step in order:
            @pl.when(turn(peer(step), a) == h)
            def _(step=step):
                for cut in range(cuts):
                    plane_copy(cuts * a + cut, step).start()
        for step in order:
            @pl.when((peer(step) // 2 == a) & (h == 1))
            def _(step=step):
                plane_copy(extra, step).start()

    def gather(i):
        t, a = chunk(i)
        for step in order:
            plane_copy(t, nq - step).wait_recv()
        rows, cols = corner(t, q)
        recv[0, t] = s_ref[rows, cols]
        for w in range(NWIN):
            total = jnp.zeros((CUT, LANES), jnp.float32)
            for s in range(nq):
                total = total + small[s, groups + w:groups + w + 1, :] * recv[s, t]
            part[t, w] = total

        @pl.when((z == 0) & (a > z))
        def _():
            up_copy(t).start()

        @pl.when((z == nz - 1) & (a < z))
        def _():
            down_copy(t).start()

    def relay(i):
        t, a = chunk(i)

        @pl.when((z > 0) & (a > z))
        def _():
            up_copy(t).wait_recv()
            part[t] = part[t] + from_lo[t]
            up_copy(t).start()

        @pl.when((z < nz - 1) & (a < z))
        def _():
            down_copy(t).wait_recv()
            part[t] = part[t] + from_hi[t]
            down_copy(t).start()

    def finish(i):
        t, a = chunk(i)

        @pl.when(a == z)
        def _():
            @pl.when(z > 0)
            def _():
                up_copy(t).wait_recv()
                part[t] = part[t] + from_lo[t]

            @pl.when(z < nz - 1)
            def _():
                down_copy(t).wait_recv()
                part[t] = part[t] + from_hi[t]

            @pl.when(t == extra)
            def _():
                swap_copy(core).start()

            @pl.when(t != extra)
            def _():
                cut = lax.rem(t, cuts)

                @pl.when(chip != z)
                def _():
                    mirror_copy(cut).start()
                row = turn(q, z) * LANES + cut * CUT
                out_ref[:, pl.ds(pl.multiple_of(row, CUT), CUT), :] = part[t]

    def small_sums():
        small[0] = own[...]
        for step in range(1, nq):
            small_copy(nq - step).wait_recv()
        for w in range(NWIN):
            total = jnp.zeros((groups, LANES), jnp.float32)
            for s in range(nq):
                total = total + small[s, groups + w:groups + w + 1, :] * small[s, :groups, :]
            rsum[w] = total
        for step in range(1, nz):
            rhs_copy(step).start()

    lax.fori_loop(0, AHEAD, lambda i, carry: (send(i), carry)[1], 0)
    small_sums()

    def body(i, carry):
        @pl.when(i + AHEAD < steps)
        def _():
            send(i + AHEAD)

        @pl.when(i <= extra)
        def _():
            gather(i)

        @pl.when(i >= LAG)
        def _():
            relay(i - LAG)

        @pl.when(i <= extra)
        def _():
            finish(i)
        return carry

    lax.fori_loop(0, extra + 1 + LAG, body, 0)

    for step in range(1, nz):
        rhs_copy(nz - step).wait_recv()
    total = rsum[...]
    for step in range(1, nz):
        total = total + rrecv[step]
    rrecv[0] = total
    for w in range(NWIN):
        for h in range(2):
            rhs_ref[w:w + 1, h * LANES:(h + 1) * LANES] = rrecv[0, w, pl.ds(2 * z + h, 1), :]

    @pl.when(chip != z)
    def _():
        for cut in range(cuts):
            mirror_copy(cut).wait_recv()
        row = (1 - turn(q, z)) * LANES
        for w in range(NWIN):
            block = jnp.concatenate([mirror[cut, w] for cut in range(cuts)], axis=0)
            out_ref[w, pl.ds(pl.multiple_of(row, LANES), LANES), :] = block.T

    for side in range(2):
        @pl.when((chip == z) & (core == side))
        def _(side=side):
            swap_copy(1 - side).wait_recv()
            for w in range(NWIN):
                pieces = [part[extra, w] if cut == side else mirror[cut, w] for cut in range(cuts)]
                block = jnp.concatenate(pieces, axis=0)
                out_ref[w, (1 - side) * LANES:(2 - side) * LANES, :] = block.T if side else block

    for step in range(1, nq):
        small_copy(step).wait_send()
    for step in range(1, nz):
        rhs_copy(step).wait_send()

    @pl.when(chip != z)
    def _():
        for cut in range(cuts):
            mirror_copy(cut).wait_send()

    @pl.when(chip == z)
    def _():
        swap_copy(core).wait_send()

    def drain(t, carry):
        for step in range(1, nq):
            plane_copy(t, step).wait_send()
        a = jnp.where(t == extra, chip, t // cuts)

        @pl.when(a != z)
        def _():
            up_copy(t).wait_send()
        return carry

    lax.fori_loop(0, extra + 1, drain, 0)


def assemble(nq, nz, count, window, local_b, global_b, resid, weight):
    slots, params = global_b.shape
    size = local_b.shape[1]
    groups = params // LANES
    cuts = LANES // CUT
    chunks = cuts * nz + 1
    smem = pl.BlockSpec(memory_space=pltpu.SMEM)
    hbm = pl.BlockSpec(memory_space=pltpu.HBM)
    vmem = pl.BlockSpec(memory_space=pltpu.VMEM)
    f32, bf16 = jnp.float32, jnp.bfloat16
    block = pltpu.VMEM((chunks, NWIN, CUT, LANES), f32)
    dma = pltpu.SemaphoreType.DMA
    return pl.pallas_call(
        functools.partial(assemble_kernel, nq, nz),
        out_shape=(jax.ShapeDtypeStruct((NWIN, params // nz, LANES), f32),
                   jax.ShapeDtypeStruct((NWIN, params // nz), f32)),
        in_specs=[smem, smem, hbm, hbm, hbm, hbm],
        out_specs=(vmem, vmem),
        scratch_shapes=[
            pltpu.VMEM((slots, size), f32), pltpu.VMEM((slots, params), f32),
            pltpu.VMEM((1, slots), f32), pltpu.VMEM((1, slots), f32),
            pltpu.VMEM((slots, params), bf16), pltpu.VMEM((slots, params), bf16),
            pltpu.VMEM((size, params), f32),
            pltpu.VMEM((size, params), bf16), pltpu.VMEM((size, params), bf16),
            pltpu.VMEM((size, params), bf16), pltpu.VMEM((size, params), bf16),
            pltpu.VMEM((params, params), f32),
            pltpu.VMEM((2 * groups, LANES), f32),
            pltpu.VMEM((nq, chunks, CUT, LANES), f32),
            pltpu.VMEM((nq, 2 * groups, LANES), f32),
            block, block, block,
            pltpu.VMEM((cuts, NWIN, CUT, LANES), f32),
            pltpu.VMEM((NWIN, groups, LANES), f32),
            pltpu.VMEM((nz, NWIN, groups, LANES), f32),
            dma((7,)), dma((nq, chunks)), dma((nq, chunks)), dma((nq,)), dma((nq,)),
            dma((chunks,)), dma((chunks,)), dma((chunks,)), dma((nz,)), dma((nz,)),
            dma((cuts,)), dma((cuts,)),
        ],
        compiler_params=pltpu.CompilerParams(
            collective_id=0, has_side_effects=True, vmem_limit_bytes=48 * 1024 * 1024),
        name="assemble",
    )(count, window, local_b, global_b, resid, weight)


def reduced_bundle(local_b, global_b, resid_b, weight_b, count):
    measure_slot, local_param = local_b.shape
    slots = jnp.arange(measure_slot, dtype=jnp.int32)
    live = jnp.where(slots < count, weight_b, jnp.float32(0.0))
    root = jnp.sqrt(live)[:, None]
    ls = local_b * root
    gs = global_b * root
    rs = resid_b[:, None] * root
    curv = tdot(ls, ls) + jnp.eye(local_param, dtype=jnp.float32)
    coupling = tdot(ls, gs)
    lr = tdot(ls, rs)
    gr = tdot(gs, rs)[:, 0]
    factor = jnp.linalg.cholesky(curv)
    solved_all = jax.scipy.linalg.cho_solve((factor, True), jnp.concatenate([coupling, lr], axis=1))
    solved, solved_rhs = solved_all[:, :-1], solved_all[:, -1:]
    schur = tdot(gs, gs, HIGH) - tdot(coupling, solved, HIGH)
    reduced = gr - tdot(coupling, solved_rhs)[:, 0]
    return schur, reduced


def on_device(local_slopes, global_slopes, residuals, weights, track_slot_count, windows):
    nq, nz = lax.axis_size("wide"), lax.axis_size("narrow")
    slots, params = global_slopes.shape[1:]
    owned = params // nz
    z = lax.axis_index("narrow")
    if params // nq == LANES and local_slopes.shape[2] == LANES and nq == 2 * nz and nz > 1:
        return assemble(nq, nz, track_slot_count, windows, local_slopes[0], global_slopes[0], residuals, weights)
    schur, reduced = reduced_bundle(
        local_slopes[0], global_slopes[0], residuals[0], weights[0], track_slot_count[0])
    picks = (windows[0] == jnp.arange(NWIN, dtype=jnp.int32)).astype(jnp.float32)
    rhs_whole = lax.psum(picks[:, None] * reduced[None], ("wide", "narrow"))
    normal_rhs = lax.dynamic_slice_in_dim(rhs_whole, z * owned, owned, 1)
    received = lax.all_to_all(schur[None], "wide", split_axis=2, concat_axis=0, tiled=True)
    all_picks = lax.all_gather(picks, "wide", axis=0)
    partial_value = jnp.einsum("bw,bij->wij", all_picks, received, precision=HIGHEST,
                               preferred_element_type=jnp.float32)
    return lax.psum_scatter(partial_value, "narrow", scatter_dimension=1, tiled=True), normal_rhs


def solution(mesh):
    in_specs = (
        P(("wide", "narrow"), None, None),
        P(("wide", "narrow"), None, None),
        P(("wide", "narrow"), None),
        P(("wide", "narrow"), None),
        P(("wide", "narrow")),
        P(("wide", "narrow")),
    )
    out_specs = (P(None, "narrow", "wide"), P(None, "narrow"))
    return jax.shard_map(
        on_device, mesh=mesh, in_specs=in_specs, out_specs=out_specs, check_vma=False
    )
```

time: 86 us -> 67.6 us (0.79)
  the two profiles are of different devices: /device:TPU:31 before, /device:TPU:29 now
where the time goes in v1:
time: 67.6 us; the launch traced here: 67.4 us
  Pallas kernels  60.2 us (89%)
  local copies, waits for them, and re-layouts  5.28 us (8%)
  between operations  1.94 us (3%)
    pallas_call x1, Pallas kernels, assemble(): pl.pallas_call(functools.partial(assemble_kernel, nq, nz), out_shape=(jax...  60.2 us
    unnamed x10, local copies, waits for them, and re-layouts  5.28 us

profile of v1, /device:TPU:29, one launch (start us, length us, event | category | flops | bytes accessed | tf_op | source)
XLA Modules:
  0.0 67.4 jit_solution(18314025513905344437)
XLA Ops:
  1.9 0.0 copy-start
  1.9 1.6 %copy-done = f32[1,512,1024]{2,1,0:T(8,128)S(1)} copy-done((f32[1,512,1024]{2,1,0:T(8,128)S(1)}, f32[1,512,1024]{2,1,0:T(8,128)}, u32[]{:S(2)}) %copy-start) | copy-done | bytes 2097176
  3.5 0.0 copy-start.1
  3.5 0.9 %copy-done.1 = f32[1,512,128]{2,1,0:T(8,128)S(1)} copy-done((f32[1,512,128]{2,1,0:T(8,128)S(1)}, f32[1,512,128]{2,1,0:T(8,128)}, u32[]{:S(2)}) %copy-start.1) | copy-done | bytes 262168
  4.5 0.0 copy-start.2
  4.5 0.7 %copy-done.2 = f32[1,512]{1,0:T(1,128)S(1)} copy-done((f32[1,512]{1,0:T(1,128)S(1)}, f32[1,512]{1,0:T(1,128)}, u32[]{:S(2)}) %copy-start.2) | copy-done | bytes 2072
  5.1 0.0 copy-start.3
  5.1 0.7 %copy-done.3 = f32[1,512]{1,0:T(1,128)S(1)} copy-done((f32[1,512]{1,0:T(1,128)S(1)}, f32[1,512]{1,0:T(1,128)}, u32[]{:S(2)}) %copy-start.3) | copy-done | bytes 2072
  5.8 60.2 %assemble.1 = (f32[4,256,128]{2,1,0:T(8,128)S(1)}, f32[4,256]{1,0:T(4,128)S(1)}) custom-call(s32[1]{0:T(128)S(6)} %copy.10.count_ref, s32[1]{0:T(128)S(6)} %copy.11.window_ref, f32[512,128]{1,0:T(8,128)S(1)} %bitcast.3, f32[512,1024]{1,0:T(8,128)S(1)} %bitcast.2, f32[1,512]{1,0:T(1,128)S(1)} %copy-done.2, f32[1,512]{1,0:T(1,128)S(1)} %copy-done.3), custom_call_target="tpu_custom_call" | custom-call | tf_op jit(solution)/shard_map/assemble/pallas_call | solution.py:437
  66.0 0.8 %copy.12 = f32[4,256,128]{2,1,0:T(8,128)} copy(f32[4,256,128]{2,1,0:T(8,128)S(1)} %get-tuple-element.4) | data formatting | bytes 1048576
  66.8 0.6 copy.13
Async XLA Ops:
  1.9 1.6 %copy-start = (f32[1,512,1024]{2,1,0:T(8,128)S(1)}, f32[1,512,1024]{2,1,0:T(8,128)}, u32[]{:S(2)}) copy-start(f32[1,512,1024]{2,1,0:T(8,128)} %param.7) | copy-start | bytes 6291460
  3.5 0.9 %copy-start.1 = (f32[1,512,128]{2,1,0:T(8,128)S(1)}, f32[1,512,128]{2,1,0:T(8,128)}, u32[]{:S(2)}) copy-start(f32[1,512,128]{2,1,0:T(8,128)} %param.6) | copy-start | bytes 786436
  4.5 0.7 %copy-start.2 = (f32[1,512]{1,0:T(1,128)S(1)}, f32[1,512]{1,0:T(1,128)}, u32[]{:S(2)}) copy-start(f32[1,512]{1,0:T(1,128)} %resid_hbm.1) | copy-start | bytes 6148
  5.1 0.7 %copy-start.3 = (f32[1,512]{1,0:T(1,128)S(1)}, f32[1,512]{1,0:T(1,128)}, u32[]{:S(2)}) copy-start(f32[1,512]{1,0:T(1,128)} %weight_hbm.1) | copy-start | bytes 6148

commit v2 on v1

--- a/solution.py
+++ b/solution.py
@@ -10,10 +10,11 @@
 NWIN = 4
 LANES = 128
 SUB = 8
-PANEL = 64
+PANEL = 32
 CUT = 64
-AHEAD = 2
+AHEAD = 4
 LAG = 1
+SETTLE = 3
 MESH = pl.DeviceIdType.MESH
 HIGHEST = lax.Precision.HIGHEST
 HIGH = lax.Precision.HIGH
@@ -71,21 +72,19 @@
     return jnp.concatenate(rows, axis=0)
 
 
-def invert(c):
+def invert_panel(c, base):
     size = c.shape[0]
     lane = lax.broadcasted_iota(jnp.int32, (1, size), 1)
-    for base in range(0, size, PANEL):
-        end = base + PANEL
-        panel = eliminate([c[i:i + SUB, :] for i in range(base, end, SUB)], base)
-
-        def framed(above, below):
-            return jnp.concatenate([x for x in (above, panel, below) if x.shape[0]], axis=0)
-
-        heads = framed(jnp.zeros((base, size), jnp.float32), jnp.zeros((size - end, size), jnp.float32))
-        taken = jnp.dot(c, heads, precision=HIGHEST, preferred_element_type=jnp.float32)
-        rest = jnp.where((lane >= base) & (lane < end), 0.0, c) - taken
-        c = framed(rest[:base, :], rest[end:, :])
-    return c
+    end = base + PANEL
+    panel = eliminate([c[i:i + SUB, :] for i in range(base, end, SUB)], base)
+
+    def framed(above, below):
+        return jnp.concatenate([x for x in (above, panel, below) if x.shape[0]], axis=0)
+
+    heads = framed(jnp.zeros((base, size), jnp.float32), jnp.zeros((size - end, size), jnp.float32))
+    taken = jnp.dot(c, heads, precision=HIGHEST, preferred_element_type=jnp.float32)
+    rest = jnp.where((lane >= base) & (lane < end), 0.0, c) - taken
+    return framed(rest[:base, :], rest[end:, :])
 
 
 def split(x):
@@ -104,9 +103,9 @@
 def assemble_kernel(nq, nz, count_ref, window_ref, local_hbm, global_hbm, resid_hbm, weight_hbm,
                     out_ref, rhs_ref,
                     ls_ref, gs_ref, resid_ref, weight_ref, high, low, u_ref, u_high, u_low, x_high, x_low,
-                    s_ref, own, recv, small, part, from_lo, from_hi, mirror, rsum, rrecv,
+                    s_ref, own, recv, small, part, from_lo, from_hi, mirror, hold, rsum, rrecv,
                     in_sem, send_sem, recv_sem, small_send, small_recv,
-                    z_send, lo_sem, hi_sem, r_send, r_recv, m_send, m_recv):
+                    z_send, lo_sem, hi_sem, r_send, r_recv, m_send, m_recv, h_send, h_recv):
     q = lax.axis_index("wide")
     z = lax.axis_index("narrow")
     slots, params = gs_ref.shape
@@ -134,7 +133,7 @@
             if dz or step:
                 pl.semaphore_signal(barrier, inc=1, device_id=(peer(step), lax.rem(z + dz, nz)),
                                     device_id_type=MESH)
-    for copy in loads:
+    for copy in loads[:3]:
         copy.wait()
 
     slot = lax.broadcasted_iota(jnp.int32, (1, slots), 1)
@@ -149,21 +148,29 @@
     lr = jnp.sum(ls * rs_col, axis=0, keepdims=True)
     lr_col = jnp.broadcast_to(lr, (LANES, size)).T
     ls_high, ls_low = split(ls_t)
-    for g in range(groups):
-        cols = slice(g * LANES, (g + 1) * LANES)
-        gs = gs_ref[:, cols] * root_col
-        gs_high, gs_low = split(gs)
-        high[:, cols], low[:, cols] = gs_high, gs_low
-        own[g:g + 1, :] = jnp.sum(gs * rs_col, axis=0, keepdims=True)
-    inverse = invert(curv)
     wide = 2 * LANES
-    for g in range(0, params, wide):
-        cols = slice(g, g + wide)
-        coupling = (jnp.dot(ls_high, high[:, cols], preferred_element_type=jnp.float32)
-                    + (jnp.dot(ls_high, low[:, cols], preferred_element_type=jnp.float32)
-                       + jnp.dot(ls_low, high[:, cols], preferred_element_type=jnp.float32)))
-        u_ref[:, cols] = coupling
-        u_high[:, cols], u_low[:, cols] = split(coupling)
+
+    def couple():
+        for g in range(groups):
+            cols = slice(g * LANES, (g + 1) * LANES)
+            gs = gs_ref[:, cols] * root_col
+            high[:, cols], low[:, cols] = split(gs)
+            own[g:g + 1, :] = jnp.sum(gs * rs_col, axis=0, keepdims=True)
+        for g in range(0, params, wide):
+            cols = slice(g, g + wide)
+            coupling = (jnp.dot(ls_high, high[:, cols], preferred_element_type=jnp.float32)
+                        + (jnp.dot(ls_high, low[:, cols], preferred_element_type=jnp.float32)
+                           + jnp.dot(ls_low, high[:, cols], preferred_element_type=jnp.float32)))
+            u_ref[:, cols] = coupling
+            u_high[:, cols], u_low[:, cols] = split(coupling)
+
+    inverse = invert_panel(curv, 0)
+    for copy in loads[3:]:
+        copy.wait()
+    couple()
+    for base in range(PANEL, size, PANEL):
+        inverse = invert_panel(inverse, base)
+
     for g in range(0, params, wide):
         cols = slice(g, g + wide)
         solved = jnp.dot(inverse, u_ref[:, cols], precision=HIGHEST, preferred_element_type=jnp.float32)
@@ -174,7 +181,7 @@
                 solved[:, h * LANES:(h + 1) * LANES] * lr_col, axis=0, keepdims=True)
     own[groups:, :] = (lax.broadcasted_iota(jnp.int32, (groups, LANES), 0) == window_ref[0]).astype(jnp.float32)
 
-    orders = [sorted(range(nz), key=lambda a: (-abs(a - i), a if i >= nz // 2 else -a)) for i in range(nz)]
+    orders = [sorted(range(nz), key=lambda a: (min(a, nz - 1 - a), -abs(a - i))) for i in range(nz)]
 
     def goal(k):
         a = jnp.int32(0)
@@ -191,6 +198,10 @@
         return k
 
     late = cuts * place(chip) + cuts
+
+    def final(i):
+        plain = jnp.where(i > late, i - 1, i)
+        return jnp.where(i == late, place(chip), jnp.minimum(plain // cuts, nz - 1)) == nz - 1
 
     def chunk(i):
         plain = jnp.where(i > late, i - 1, i)
@@ -242,6 +253,27 @@
         return pltpu.make_async_remote_copy(
             src_ref=part.at[cuts * z + cut], dst_ref=mirror.at[cut], send_sem=m_send.at[cut], recv_sem=m_recv.at[cut],
             device_id=(2 * z + turn(q, z), chip), device_id_type=MESH)
+
+    def hold_copy():
+        return pltpu.make_async_remote_copy(
+            src_ref=part.at[cuts * z], dst_ref=hold.at[chip], send_sem=m_send.at[0], recv_sem=h_recv.at[chip],
+            device_id=(2 * z + turn(q, z), z), device_id_type=MESH)
+
+    def forward_copy(a):
+        return pltpu.make_async_remote_copy(
+            src_ref=hold.at[a], dst_ref=mirror.at[0], send_sem=h_send.at[a], recv_sem=m_recv.at[0],
+            device_id=(q, a), device_id_type=MESH)
+
+    def arrived(a):
+        return pltpu.make_async_remote_copy(
+            src_ref=part.at[cuts * z], dst_ref=hold.at[a], send_sem=m_send.at[0], recv_sem=h_recv.at[a],
+            device_id=(2 * z + turn(q, z), z), device_id_type=MESH)
+
+    def forward(a):
+        @pl.when((chip == z) & (z != a))
+        def _():
+            arrived(a).wait_recv()
+            forward_copy(a).start()
 
     def swap_copy(cut):
         return pltpu.make_async_remote_copy(
@@ -326,7 +358,11 @@
             def _():
                 cut = lax.rem(t, cuts)
 
-                @pl.when(chip != z)
+                @pl.when((chip != z) & (cut == 0))
+                def _():
+                    hold_copy().start()
+
+                @pl.when((chip != z) & (cut != 0))
                 def _():
                     mirror_copy(cut).start()
                 row = turn(q, z) * LANES + cut * CUT
@@ -360,12 +396,24 @@
         def _():
             relay(i - LAG)
 
-        @pl.when(i <= extra)
+        @pl.when((i >= SETTLE) & jnp.logical_not(final(i - SETTLE)))
+        def _():
+            finish(i - SETTLE)
+
+        @pl.when((i <= extra) & final(i))
         def _():
             finish(i)
+
+        for g in range(nz // 2 - 1):
+            @pl.when(i == 2 * cuts * (g + 1) + SETTLE + 2)
+            def _(g=g):
+                forward(g)
+                forward(nz - 1 - g)
         return carry
 
     lax.fori_loop(0, extra + 1 + LAG, body, 0)
+    for a in range(nz // 2 - 1, nz - nz // 2 + 1):
+        forward(a)
 
     for step in range(1, nz):
         rhs_copy(nz - step).wait_recv()
@@ -408,6 +456,10 @@
     @pl.when(chip == z)
     def _():
         swap_copy(core).wait_send()
+        for a in range(nz):
+            @pl.when(z != a)
+            def _(a=a):
+                forward_copy(a).wait_send()
 
     def drain(t, carry):
         for step in range(1, nq):
@@ -438,7 +490,7 @@
         functools.partial(assemble_kernel, nq, nz),
         out_shape=(jax.ShapeDtypeStruct((NWIN, params // nz, LANES), f32),
                    jax.ShapeDtypeStruct((NWIN, params // nz), f32)),
-        in_specs=[smem, smem, hbm, hbm, hbm, hbm],
+        in_specs=[smem] * 2 + [hbm] * 4,
         out_specs=(vmem, vmem),
         scratch_shapes=[
             pltpu.VMEM((slots, size), f32), pltpu.VMEM((slots, params), f32),
@@ -452,17 +504,17 @@
             pltpu.VMEM((nq, chunks, CUT, LANES), f32),
             pltpu.VMEM((nq, 2 * groups, LANES), f32),
             block, block, block,
-            pltpu.VMEM((cuts, NWIN, CUT, LANES), f32),
+            pltpu.VMEM((cuts, NWIN, CUT, LANES), f32), pltpu.VMEM((nz, NWIN, CUT, LANES), f32),
             pltpu.VMEM((NWIN, groups, LANES), f32),
             pltpu.VMEM((nz, NWIN, groups, LANES), f32),
             dma((7,)), dma((nq, chunks)), dma((nq, chunks)), dma((nq,)), dma((nq,)),
             dma((chunks,)), dma((chunks,)), dma((chunks,)), dma((nz,)), dma((nz,)),
-            dma((cuts,)), dma((cuts,)),
+            dma((cuts,)), dma((cuts,)), dma((nz,)), dma((nz,)),
         ],
         compiler_params=pltpu.CompilerParams(
             collective_id=0, has_side_effects=True, vmem_limit_bytes=48 * 1024 * 1024),
         name="assemble",
-    )(count, window, local_b, global_b, resid, weight)
+    )(count, window, *(pltpu.with_memory_space_constraint(x, pltpu.HBM) for x in (local_b, global_b, resid, weight)))
 
 
 def reduced_bundle(local_b, global_b, resid_b, weight_b, count):

time: 67.6 us -> 58.8 us (0.87)
  the two profiles are of different devices: /device:TPU:29 before, /device:TPU:13 now
where the time goes in v2:
time: 58.8 us; the launch traced here: 58.6 us
  Pallas kernels  55.3 us (94%)
  between operations  1.93 us (3%)
  local copies, waits for them, and re-layouts  1.39 us (2%)
    pallas_call x1, Pallas kernels, assemble(): pl.pallas_call(functools.partial(assemble_kernel, nq, nz), out_shape=(jax...  55.3 us
    unnamed x2, local copies, waits for them, and re-layouts  1.39 us

profile of v2, /device:TPU:13, one launch (start us, length us, event | category | flops | bytes accessed | tf_op | source)
XLA Modules:
  0.0 58.6 jit_solution(5917877106807118089)
XLA Ops:
  1.9 55.3 %assemble.1 = (f32[4,256,128]{2,1,0:T(8,128)S(1)}, f32[4,256]{1,0:T(4,128)S(1)}) custom-call(s32[1]{0:T(128)S(6)} %copy.10.count_ref, s32[1]{0:T(128)S(6)} %copy.11.window_ref, f32[512,128]{1,0:T(8,128)} %bitcast.3, f32[512,1024]{1,0:T(8,128)} %bitcast.2, f32[1,512]{1,0:T(1,128)} %resid_hbm.1, f32[1,512]{1,0:T(1,128)} %weight_hbm.1), custom_call_target="tpu_custom_call" | custom-call | tf_op jit(solution)/shard_map/assemble/pallas_call | solution.py:489
  57.3 0.8 %copy.12 = f32[4,256,128]{2,1,0:T(8,128)} copy(f32[4,256,128]{2,1,0:T(8,128)S(1)} %get-tuple-element.4) | data formatting | bytes 1048576
  58.1 0.6 %copy.13 = f32[4,256]{1,0:T(4,128)} copy(f32[4,256]{1,0:T(4,128)S(1)} %get-tuple-element.5) | data formatting | bytes 8192

commit v3 on v2

--- a/solution.py
+++ b/solution.py
@@ -15,6 +15,8 @@
 AHEAD = 4
 LAG = 1
 SETTLE = 3
+HOP = 3
+MIRROR = -0.8
 MESH = pl.DeviceIdType.MESH
 HIGHEST = lax.Precision.HIGHEST
 HIGH = lax.Precision.HIGH
@@ -181,20 +183,49 @@
                 solved[:, h * LANES:(h + 1) * LANES] * lr_col, axis=0, keepdims=True)
     own[groups:, :] = (lax.broadcasted_iota(jnp.int32, (groups, LANES), 0) == window_ref[0]).astype(jnp.float32)
 
-    orders = [sorted(range(nz), key=lambda a: (min(a, nz - 1 - a), -abs(a - i))) for i in range(nz)]
+    def urgency(i, c, a):
+        return HOP * abs(i - a) + (MIRROR + abs(a - c) * 0.2 if a != c else 0)
+
+    plans = [[sorted(range(nz), key=lambda a: (-urgency(i, c, a), a)) for c in range(nz)] for i in range(nz)]
+    rows_by = [sorted(range(nz), key=lambda a: (sum(plan.index(a) for plan in plans[i]), abs(2 * a - nz + 1) * -1, a)) for i in range(nz)]
+    sent_at = [[[max(rows_by[i].index(x) for x in plan[:k + 1]) for k in range(nz)] for plan in plans[i]]
+               for i in range(nz)]
+
+    assert all(2 * x + 1 <= 2 * k + AHEAD for rows in sent_at for row in rows for k, x in enumerate(row))
+
+    def here(values):
+        total = jnp.int32(0)
+        for i in range(nz):
+            total = total + jnp.where(z == i, values[i], 0)
+        return total
+
+    plan = [[here([plans[i][c][k] for i in range(nz)]) for k in range(nz)] for c in range(nz)]
+    group = [[here([sent_at[i][c][k] for i in range(nz)]) for k in range(nz)] for c in range(nz)]
+    ways = [3, 1, 2, 0] if nz == 4 else list(range(nz - 1, -1, -1))
+    aims = [lax.rem(chip + d, nz) for d in ways]
+    plan_to = [[sum(jnp.where(aim == c, plan[c][k], 0) for c in range(nz)) for k in range(nz)] for aim in aims]
+    group_to = [[sum(jnp.where(aim == c, group[c][k], 0) for c in range(nz)) for k in range(nz)] for aim in aims]
+    row_plan = [here([rows_by[i][k] for i in range(nz)]) for k in range(nz)]
+    mine = []
+    for k in range(nz):
+        total = jnp.int32(0)
+        for c in range(nz):
+            total = total + jnp.where(chip == c, plan[c][k], 0)
+        mine.append(total)
+
+    def pick(values, k):
+        total = jnp.int32(0)
+        for j in range(nz):
+            total = total + jnp.where(k == j, values[j], 0)
+        return total
 
     def goal(k):
-        a = jnp.int32(0)
-        for i in range(nz):
-            for j in range(nz):
-                a = a + jnp.where((z == i) & (k == j), orders[i][j], 0)
-        return a
+        return pick(mine, k)
 
     def place(a):
         k = jnp.int32(0)
-        for i in range(nz):
-            for j in range(nz):
-                k = k + jnp.where((z == i) & (a == orders[i][j]), j, 0)
+        for j in range(nz):
+            k = k + jnp.where(a == mine[j], j, 0)
         return k
 
     late = cuts * place(chip) + cuts
@@ -286,19 +317,28 @@
         small_copy(step).start()
 
     def send(i):
-        a, h = goal(i // 2), lax.rem(i, 2)
-        block = pl.ds(pl.multiple_of((2 * a + h) * LANES, LANES), LANES)
+        j, h = i // 2, lax.rem(i, 2)
+        now = pick(row_plan, j)
+        block = pl.ds(pl.multiple_of((2 * now + h) * LANES, LANES), LANES)
         s_ref[block, :] = (three(high[:, block], low[:, block], high[...], low[...])
                            - three(u_high[:, block], u_low[:, block], x_high[...], x_low[...]))
-        for step in order:
-            @pl.when(turn(peer(step), a) == h)
-            def _(step=step):
-                for cut in range(cuts):
-                    plane_copy(cuts * a + cut, step).start()
-        for step in order:
-            @pl.when((peer(step) // 2 == a) & (h == 1))
-            def _(step=step):
-                plane_copy(extra, step).start()
+        for d, c in enumerate(aims):
+            for k in range(nz):
+                a = plan_to[d][k]
+
+                @pl.when(group_to[d][k] == j)
+                def _(a=a, c=c):
+                    for side in range(2):
+                        col = 2 * c + side
+
+                        @pl.when((q != col) & (jnp.where(a == now, turn(col, a), 0) == h))
+                        def _(col=col):
+                            for cut in range(cuts):
+                                plane_copy(cuts * a + cut, lax.rem(col + nq - q, nq)).start()
+
+                        @pl.when((q != col) & (a == c) & (jnp.where(a == now, 1, 0) == h))
+                        def _(col=col):
+                            plane_copy(extra, lax.rem(col + nq - q, nq)).start()
 
     def gather(i):
         t, a = chunk(i)
@@ -404,15 +444,10 @@
         def _():
             finish(i)
 
-        for g in range(nz // 2 - 1):
-            @pl.when(i == 2 * cuts * (g + 1) + SETTLE + 2)
-            def _(g=g):
-                forward(g)
-                forward(nz - 1 - g)
         return carry
 
     lax.fori_loop(0, extra + 1 + LAG, body, 0)
-    for a in range(nz // 2 - 1, nz - nz // 2 + 1):
+    for a in range(nz):
         forward(a)
 
     for step in range(1, nz):

time: 58.8 us -> 55.4 us (0.942)
  the two profiles are of different devices: /device:TPU:13 before, /device:TPU:22 now
where the time goes in v3:
time: 55.4 us; the launch traced here: 55.2 us
  Pallas kernels  51.9 us (94%)
  between operations  1.93 us (3%)
  local copies, waits for them, and re-layouts  1.39 us (3%)
    pallas_call x1, Pallas kernels, assemble(): pl.pallas_call(functools.partial(assemble_kernel, nq, nz), out_shape=(jax...  51.9 us
    unnamed x2, local copies, waits for them, and re-layouts  1.39 us

profile of v3, /device:TPU:22, one launch (start us, length us, event | category | flops | bytes accessed | tf_op | source)
XLA Modules:
  0.0 55.2 jit_solution(7324590480194314205)
XLA Ops:
  1.9 51.9 %assemble.1 = (f32[4,256,128]{2,1,0:T(8,128)S(1)}, f32[4,256]{1,0:T(4,128)S(1)}) custom-call(s32[1]{0:T(128)S(6)} %copy.10.count_ref, s32[1]{0:T(128)S(6)} %copy.11.window_ref, f32[512,128]{1,0:T(8,128)} %bitcast.3, f32[512,1024]{1,0:T(8,128)} %bitcast.2, f32[1,512]{1,0:T(1,128)} %resid_hbm.1, f32[1,512]{1,0:T(1,128)} %weight_hbm.1), custom_call_target="tpu_custom_call" | custom-call | tf_op jit(solution)/shard_map/assemble/pallas_call | solution.py:524
  53.8 0.8 %copy.12 = f32[4,256,128]{2,1,0:T(8,128)} copy(f32[4,256,128]{2,1,0:T(8,128)S(1)} %get-tuple-element.4) | data formatting | bytes 1048576
  54.6 0.6 %copy.13 = f32[4,256]{1,0:T(4,128)} copy(f32[4,256]{1,0:T(4,128)S(1)} %get-tuple-element.5) | data formatting | bytes 8192

commit v4 on v3

--- a/solution.py
+++ b/solution.py
@@ -14,6 +14,7 @@
 CUT = 64
 AHEAD = 4
 LAG = 1
+PARTS = 2
 SETTLE = 3
 HOP = 3
 MIRROR = -0.8
@@ -107,7 +108,7 @@
                     ls_ref, gs_ref, resid_ref, weight_ref, high, low, u_ref, u_high, u_low, x_high, x_low,
                     s_ref, own, recv, small, part, from_lo, from_hi, mirror, hold, rsum, rrecv,
                     in_sem, send_sem, recv_sem, small_send, small_recv,
-                    z_send, lo_sem, hi_sem, r_send, r_recv, m_send, m_recv, h_send, h_recv):
+                    z_send, lo_sem, hi_sem, r_send, r_recv, m_send, m_recv, h_send, h_recv, m_half, m_part):
     q = lax.axis_index("wide")
     z = lax.axis_index("narrow")
     slots, params = gs_ref.shape
@@ -166,11 +167,11 @@
             u_ref[:, cols] = coupling
             u_high[:, cols], u_low[:, cols] = split(coupling)
 
-    inverse = invert_panel(curv, 0)
+    inverse = invert_panel(invert_panel(curv, 0), PANEL)
     for copy in loads[3:]:
         copy.wait()
     couple()
-    for base in range(PANEL, size, PANEL):
+    for base in range(2 * PANEL, size, PANEL):
         inverse = invert_panel(inverse, base)
 
     for g in range(0, params, wide):
@@ -285,26 +286,30 @@
             src_ref=part.at[cuts * z + cut], dst_ref=mirror.at[cut], send_sem=m_send.at[cut], recv_sem=m_recv.at[cut],
             device_id=(2 * z + turn(q, z), chip), device_id_type=MESH)
 
-    def hold_copy():
-        return pltpu.make_async_remote_copy(
-            src_ref=part.at[cuts * z], dst_ref=hold.at[chip], send_sem=m_send.at[0], recv_sem=h_recv.at[chip],
+    def share(p):
+        return pl.ds(p * (NWIN // PARTS), NWIN // PARTS)
+
+    def arrived(a, p):
+        return pltpu.make_async_remote_copy(
+            src_ref=part.at[cuts * z, share(p)], dst_ref=hold.at[a, share(p)],
+            send_sem=m_half.at[p], recv_sem=h_recv.at[a, p],
             device_id=(2 * z + turn(q, z), z), device_id_type=MESH)
 
-    def forward_copy(a):
-        return pltpu.make_async_remote_copy(
-            src_ref=hold.at[a], dst_ref=mirror.at[0], send_sem=h_send.at[a], recv_sem=m_recv.at[0],
+    def hold_copy(p):
+        return arrived(chip, p)
+
+    def forward_copy(a, p):
+        return pltpu.make_async_remote_copy(
+            src_ref=hold.at[a, share(p)], dst_ref=mirror.at[0, share(p)],
+            send_sem=h_send.at[a, p], recv_sem=m_part.at[p],
             device_id=(q, a), device_id_type=MESH)
-
-    def arrived(a):
-        return pltpu.make_async_remote_copy(
-            src_ref=part.at[cuts * z], dst_ref=hold.at[a], send_sem=m_send.at[0], recv_sem=h_recv.at[a],
-            device_id=(2 * z + turn(q, z), z), device_id_type=MESH)
 
     def forward(a):
         @pl.when((chip == z) & (z != a))
         def _():
-            arrived(a).wait_recv()
-            forward_copy(a).start()
+            for p in range(PARTS):
+                arrived(a, p).wait_recv()
+                forward_copy(a, p).start()
 
     def swap_copy(cut):
         return pltpu.make_async_remote_copy(
@@ -400,7 +405,8 @@
 
                 @pl.when((chip != z) & (cut == 0))
                 def _():
-                    hold_copy().start()
+                    for p in range(PARTS):
+                        hold_copy(p).start()
 
                 @pl.when((chip != z) & (cut != 0))
                 def _():
@@ -462,8 +468,10 @@
 
     @pl.when(chip != z)
     def _():
-        for cut in range(cuts):
+        for cut in range(1, cuts):
             mirror_copy(cut).wait_recv()
+        for p in range(PARTS):
+            forward_copy(0, p).wait_recv()
         row = (1 - turn(q, z)) * LANES
         for w in range(NWIN):
             block = jnp.concatenate([mirror[cut, w] for cut in range(cuts)], axis=0)
@@ -485,8 +493,10 @@
 
     @pl.when(chip != z)
     def _():
-        for cut in range(cuts):
+        for cut in range(1, cuts):
             mirror_copy(cut).wait_send()
+        for p in range(PARTS):
+            hold_copy(p).wait_send()
 
     @pl.when(chip == z)
     def _():
@@ -494,7 +504,8 @@
         for a in range(nz):
             @pl.when(z != a)
             def _(a=a):
-                forward_copy(a).wait_send()
+                for p in range(PARTS):
+                    forward_copy(a, p).wait_send()
 
     def drain(t, carry):
         for step in range(1, nq):
@@ -544,7 +555,7 @@
             pltpu.VMEM((nz, NWIN, groups, LANES), f32),
             dma((7,)), dma((nq, chunks)), dma((nq, chunks)), dma((nq,)), dma((nq,)),
             dma((chunks,)), dma((chunks,)), dma((chunks,)), dma((nz,)), dma((nz,)),
-            dma((cuts,)), dma((cuts,)), dma((nz,)), dma((nz,)),
+            dma((cuts,)), dma((cuts,)), dma((nz, PARTS)), dma((nz, PARTS)), dma((PARTS,)), dma((PARTS,)),
         ],
         compiler_params=pltpu.CompilerParams(
             collective_id=0, has_side_effects=True, vmem_limit_bytes=48 * 1024 * 1024),

time: 55.4 us -> 54.2 us (0.978)
  Pallas kernels: 51.9 us -> 50.7 us
    pallas_call x1, Pallas kernels: 51.9 us -> 50.7 us  [assemble(): pl.pallas_call(functools.partial(assemble_kernel, nq, nz), out_shape=(jax...]
where the time goes in v4:
time: 54.2 us; the launch traced here: 54 us
  Pallas kernels  50.7 us (94%)
  between operations  1.93 us (4%)
  local copies, waits for them, and re-layouts  1.39 us (3%)
    pallas_call x1, Pallas kernels, assemble(): pl.pallas_call(functools.partial(assemble_kernel, nq, nz), out_shape=(jax...  50.7 us
    unnamed x2, local copies, waits for them, and re-layouts  1.39 us

profile of v4, /device:TPU:22, one launch (start us, length us, event | category | flops | bytes accessed | tf_op | source)
XLA Modules:
  0.0 54.0 jit_solution(2446745927614900838)
XLA Ops:
  1.9 50.7 %assemble.1 = (f32[4,256,128]{2,1,0:T(8,128)S(1)}, f32[4,256]{1,0:T(4,128)S(1)}) custom-call(s32[1]{0:T(128)S(6)} %copy.10.count_ref, s32[1]{0:T(128)S(6)} %copy.11.window_ref, f32[512,128]{1,0:T(8,128)} %bitcast.3, f32[512,1024]{1,0:T(8,128)} %bitcast.2, f32[1,512]{1,0:T(1,128)} %resid_hbm.1, f32[1,512]{1,0:T(1,128)} %weight_hbm.1), custom_call_target="tpu_custom_call" | custom-call | tf_op jit(solution)/shard_map/assemble/pallas_call | solution.py:535
  52.6 0.8 %copy.12 = f32[4,256,128]{2,1,0:T(8,128)} copy(f32[4,256,128]{2,1,0:T(8,128)S(1)} %get-tuple-element.4) | data formatting | bytes 1048576
  53.4 0.6 %copy.13 = f32[4,256]{1,0:T(4,128)} copy(f32[4,256]{1,0:T(4,128)S(1)} %get-tuple-element.5) | data formatting | bytes 8192
